TPU v7x, 32 devices: a whole 2x2x4 slice. The times are simulated.
32 devices in a mesh: rep: 2 (over y), seq: 4 (over z), head: 2 (over x), sub: 2 (over core).
Axes of the slice: x: 2, y: 2, z: 4, core: 2. Of those that a mesh axis runs over, the one named last changes fastest.
Arguments:
- queries: bfloat16 [8, 8192], P('rep', 'head'), parts along dimension 0, may hold values from -4.5 to 4.5
- key_cache: bfloat16 [1024, 128, 1024], P(('rep', 'seq', 'sub'), None, 'head'), parts along dimension 0, may hold values from -4.5 to 4.5
- value_cache: bfloat16 [1024, 128, 1024], P(('rep', 'seq', 'sub'), None, 'head'), parts along dimension 0, may hold values from -6 to 6
- seq_lengths: int32 [8], P('rep'), parts along dimension 0, may hold values from 513 to 32768, as said below
- slot_owner: int32 [1024], P(('rep', 'seq', 'sub')), parts along dimension 0, may hold values from 0 to 3, as said below
- slot_page: int32 [1024], P(('rep', 'seq', 'sub')), parts along dimension 0, may hold values from 0 to 255, as said below
- out_weight: bfloat16 [8192, 8192], P('head', ('seq', 'sub')), may hold values from -0.0625 to 0.0625
Outputs:
- projected: bfloat16 [8, 8192], P('rep', ('seq', 'sub')), parts along dimension 0
There are 2 independent parts, one for each index of `rep`. A program takes and returns all parts, laid end to end along the dimension named above; an argument that names none is the same for every part. Nothing has to cross between parts.
Inputs may be any that keep to these rules, and one draw needn't show every extreme that they name: `slot_owner`: every sequence holds 5 to 256 pages, and some sequence exactly 256; its pages are numbered 0 upward and each stands in exactly one cache page; every cache page is used; a sequence's pages occupy consecutive cache pages. slot_page[s] < ceil(seq_lengths[slot_owner[s]] / 128), and every page below that count is present. seq_lengths[b] lies in the last of its sequence's pages.
All inputs are finite; a program needn't handle non-finite values.
Results may differ from a plain program's by a relative error of at most 0.0055.
Values may be sent and summed in bfloat16 or wider, within the bound.
A program may use at most 64 MiB of HBM per device.

v0:
```python
import jax
import jax.numpy as jnp
from jax import lax
from jax.sharding import PartitionSpec as P

DH = 128
PAGE = 128
neg_fill = -1e30


def merged(part, axis, combine):
    gathered = jax.tree.map(lambda a: lax.all_gather(a, axis), part)

    def take(source):
        return jax.tree.map(lambda a: lax.dynamic_index_in_dim(a, source, 0, False), gathered)

    return lax.fori_loop(
        1, lax.axis_size(axis), lambda source, state: combine(state, take(source)), take(0)
    )


def spread(values, factor):
    row_count, col_count = factor.shape
    return (values.reshape(row_count, col_count, -1) * factor[:, :, None]).reshape(row_count, -1)


def merge_states(first, second):
    top_first, mass_first, out_first = first
    top_second, mass_second, out_second = second
    joined = jnp.maximum(top_first, top_second)
    scale_first = jnp.exp(top_first - joined)
    scale_second = jnp.exp(top_second - joined)
    mass_joined = mass_first * scale_first + mass_second * scale_second
    out_joined = spread(out_first, scale_first) + spread(out_second, scale_second)
    return (joined, mass_joined, out_joined)


def on_device(queries, key_cache, value_cache, seq_lengths, slot_owner, slot_page, out_weight):
    batch_rows = queries.shape[0]
    slot_count = key_cache.shape[0]
    groups_local = key_cache.shape[2] // DH
    per_group = queries.shape[1] // (groups_local * DH)
    picked = jnp.take(queries, slot_owner, axis=0).reshape(slot_count, groups_local, per_group, DH)
    key_tiles = key_cache.reshape(slot_count, PAGE, groups_local, DH)
    value_tiles = value_cache.reshape(slot_count, PAGE, groups_local, DH)
    scores = jnp.einsum("sgjd,stgd->sgjt", picked, key_tiles, preferred_element_type=jnp.float32)
    scores = scores * (1.0 / jnp.sqrt(jnp.float32(DH)))
    valid = jnp.clip(jnp.take(seq_lengths, slot_owner, axis=0) - slot_page * PAGE, 0, PAGE)
    positions = jnp.arange(PAGE, dtype=jnp.int32)
    live = (positions[None, :] < valid[:, None])[:, None, None, :]
    scores = jnp.where(live, scores, neg_fill)
    page_peak = jnp.max(scores, axis=-1)
    probs = jnp.exp(scores - page_peak[..., None]).astype(jnp.bfloat16)
    page_mass = jnp.sum(probs.astype(jnp.float32), axis=-1)
    page_out = jnp.einsum("sgjt,stgd->sgjd", probs, value_tiles, preferred_element_type=jnp.float32)
    owner_hits = slot_owner[None, :] == jnp.arange(batch_rows, dtype=jnp.int32)[:, None]
    seq_peak = jnp.max(jnp.where(owner_hits[:, :, None, None], page_peak[None], neg_fill), axis=1)
    factor = jnp.exp(page_peak - jnp.take(seq_peak, slot_owner, axis=0))
    hit_float = owner_hits.astype(jnp.float32)
    heads_local = groups_local * per_group
    seq_mass = jnp.dot(
        hit_float,
        (page_mass * factor).reshape(slot_count, heads_local),
        precision=lax.Precision.HIGHEST,
        preferred_element_type=jnp.float32,
    )
    seq_out = jnp.dot(
        hit_float,
        (page_out * factor[..., None]).reshape(slot_count, heads_local * DH),
        precision=lax.Precision.HIGHEST,
        preferred_element_type=jnp.float32,
    )
    seq_peak = seq_peak.reshape(batch_rows, heads_local)
    top_all, mass_all, out_all = merged((seq_peak, seq_mass, seq_out), ("seq", "sub"), merge_states)
    attention = spread(out_all, 1.0 / mass_all).astype(jnp.bfloat16)
    partial_out = jnp.dot(attention, out_weight, preferred_element_type=jnp.float32)
    return lax.psum(partial_out, "head").astype(jnp.bfloat16)


def solution(mesh):
    in_specs = (
        P("rep", "head"),
        P(("rep", "seq", "sub"), None, "head"),
        P(("rep", "seq", "sub"), None, "head"),
        P("rep"),
        P(("rep", "seq", "sub")),
        P(("rep", "seq", "sub")),
        P("head", ("seq", "sub")),
    )
    out_specs = P("rep", ("seq", "sub"))
    return jax.shard_map(
        on_device, mesh=mesh, in_specs=in_specs, out_specs=out_specs, check_vma=False
    )
```

profile of v0, /device:TPU:0, one launch (start us, length us, event | category | flops | bytes accessed | tf_op | source)
XLA Modules:
  0.0 78.8 jit_solution(3403634785775584727)
XLA Ops:
  0.0 1.5 %fusion.40 = (s32[1]{0:T(128)}, s32[1]{0:T(128)}, s32[1]{0:T(128)}, s32[1]{0:T(128)}) fusion(s32[4]{0:T(128)} %param.12), kind=kLoop, calls=%fused_computation.62 | loop fusion | bytes 32 | tf_op jit(solution)/shard_map/jit(_take)/gather | solution.py:48
  1.5 3.2 %fusion.36 = (s32[64]{0:T(128)S(1)}, s32[64]{0:T(128)S(1)}) fusion(s32[64]{0:T(128)} %param.14, s32[]{:T(128)} %bitcast.3, s32[]{:T(128)} %bitcast.4, s32[]{:T(128)} %bitcast.5, s32[]{:T(128)} %bitcast.6, s32[64]{0:T(128)} %param.13), kind=kLoop, calls=%fused_computation.59 | loop fusion | flops 1024 | bytes 1040 | tf_op jit(solution)/shard_map/jit(clip)/min | solution.py:48
  4.7 0.8 %gather_fusion = bf16[64,4096]{1,0:T(8,128)(2,1)S(1)} fusion(bf16[4,4096]{1,0:T(4,128)(2,1)S(1)} %copy-done, s32[1024]{0:T(1024)S(1)} %pad_clamp_fusion), kind=kCustom, calls=%fused_computation | custom fusion | bytes 1048832 | tf_op jit(solution)/shard_map/jit(_take)/gather | solution.py:43
  5.6 0.7 compare_and_fusion
  6.3 7.0 %fusion.41 = (f32[64,4,8]{2,1,0:T(4,128)S(1)}, f32[64,4,8,128]{3,2,1,0:T(8,128)S(1)}) fusion(bf16[64,4,8,128]{3,2,1,0:T(8,128)(2,1)S(1)} %bitcast.106, pred[64]{0:T(512)(128)(4,1)S(1)} %compare_and_fusion, pred[64,128]{1,0:T(8,128)(4,1)S(1)} %iota_compare_fusion, bf16[64,128,512]{2,1,0:T(8,128)(2,1)} %param.10), kind=kOutput, calls=%fused_computation.63 | convolution fusion | flops 68155392 | bytes 9977920 | tf_op jit(solution)/shard_map/sgjd,stgd->sgjt/dot_general | solution.py:46
  13.7 14.5 %all_gather.15 = f32[8,4,32]{2,1,0:T(4,128)S(1)} all-gather(f32[1,4,32]{2,1,0:T(4,128)S(1)} %all_gather_reshape.3), channel_id=1, replica_groups=mesh['rep'=2,'seq'=4,'head'=2,'sub'=2] {'seq','sub'}, dimensions={0}, use_global_device_ids=true | all-gather | bytes 4608 | tf_op jit(solution)/shard_map/all_gather | solution.py:12
  28.2 0.7 gather_fusion.1
  28.9 0.8 convert_reduce_fusion
  29.8 0.1 convolution_bitcast_fusion.1
  29.9 12.8 %all-gather.2 = f32[8,4,32]{2,1,0:T(4,128)S(1)} all-gather(f32[1,4,32]{2,1,0:T(4,128)S(1)} %convolution_bitcast_fusion.1), channel_id=2, replica_groups=mesh['rep'=2,'seq'=4,'head'=2,'sub'=2] {'seq','sub'}, dimensions={0}, use_global_device_ids=true | all-gather | bytes 4608 | tf_op jit(solution)/shard_map/all_gather | solution.py:12
  42.7 0.1 subtract_exponential_fusion.1
  42.8 4.7 %fusion.12 = f32[64,4,8,128]{3,2,1,0:T(8,128)S(1)} fusion(f32[64,4,8]{2,1,0:T(4,128)S(1)} %subtract_exponential_fusion.1, f32[64,4,8,128]{3,2,1,0:T(8,128)S(1)} %get-tuple-element.211, f32[64,4,8]{2,1,0:T(4,128)S(1)} %get-tuple-element.210, bf16[64,128,512]{2,1,0:T(8,128)(2,1)} %param.11), kind=kOutput, calls=%fused_computation.21 | convolution fusion | flops 67895296 | bytes 10502144 | tf_op jit(solution)/shard_map/sgjt,stgd->sgjd/dot_general | solution.py:55
  47.6 1.0 %convolution_bitcast_fusion = f32[1,4,4096]{2,1,0:T(4,128)S(1)} fusion(f32[8,8,32,128]{3,2,1,0:T(8,128)S(1)} %bitcast.108, s32[64]{0:T(128)S(1)} %copy-done.1), kind=kOutput, calls=%fused_computation.19 | convolution fusion | flops 12583168 | bytes 1114368 | tf_op jit(solution)/shard_map/dot_general | solution.py:67
  48.6 14.9 %all-gather.3 = f32[8,4,4096]{2,1,0:T(4,128)S(1)} all-gather(f32[1,4,4096]{2,1,0:T(4,128)S(1)} %convolution_bitcast_fusion), channel_id=3, replica_groups=mesh['rep'=2,'seq'=4,'head'=2,'sub'=2] {'seq','sub'}, dimensions={0}, use_global_device_ids=true | all-gather | bytes 589824 | tf_op jit(solution)/shard_map/all_gather | solution.py:12
  63.5 1.9 %while.19 = (s32[]{:T(128)}, f32[4,32]{1,0:T(4,128)S(1)}, f32[4,32]{1,0:T(4,128)S(1)}, f32[4,4096]{1,0:T(4,128)S(1)}, f32[8,4,32]{2,1,0:T(4,128)S(1)}, /*index=5...) while((s32[]{:T(128)}, f32[4,32]{1,0:T(4,128)S(1)}, ...), condition=%wide.region_4.5_spmd, body=%wide.region_3.4_spmd.sunk | while | flops 49925 | bytes 464023 | solution.py:17
  63.7 0.1 fusion.48
  63.9 0.1 fusion.48
  64.2 0.1 fusion.48
  64.5 0.1 fusion.48
  64.7 0.1 fusion.48
  65.0 0.1 fusion.48
  65.3 0.1 fusion.48
  65.5 4.6 %fusion.24 = f32[4,1024]{1,0:T(4,128)S(1)} fusion(bf16[4096,1024]{1,0:T(8,128)(2,1)} %param.15, f32[4,4096]{1,0:T(4,128)S(1)} %get-tuple-element.182, f32[1,4,32,128]{3,2,1,0:T(8,128)S(1)} %broadcast_bitcast_fusion.2), kind=kOutput, calls=%fused_computation.36 | convolution fusion | flops 33587200 | bytes 8536064 | tf_op jit(solution)/shard_map/dot_general | solution.py:76
  70.1 8.7 %psum.7 = bf16[4,1024]{1,0:T(4,128)(2,1)} all-reduce(f32[4,1024]{1,0:T(4,128)S(1)} %fusion.24), channel_id=1, replica_groups=mesh['rep'=2,'seq'=4,'head'=2,'sub'=2] {'head'}, use_global_device_ids=true, to_apply=%region_5.6 | all-reduce | flops 4096 | bytes 24576 | tf_op jit(solution)/shard_map/psum | solution.py:77
  (32 shorter events, 1.5 us)
Async XLA Ops:
  0.0 4.7 %copy-start = (bf16[4,4096]{1,0:T(4,128)(2,1)S(1)}, bf16[4,4096]{1,0:T(4,128)(2,1)}, u32[]{:S(2)}) copy-start(bf16[4,4096]{1,0:T(4,128)(2,1)} %param.9) | copy-start | bytes 98308
  0.0 13.5 %copy-start.1 = (s32[64]{0:T(128)S(1)}, s32[64]{0:T(128)}, u32[]{:S(2)}) copy-start(s32[64]{0:T(128)} %param.13) | copy-start | bytes 772
where the time goes:
time: 79.1 us; the launch traced here: 78.8 us
  blocking collectives  50.9 us (64%)
  matrix products  17.5 us (22%)
  other arithmetic  6.07 us (8%)
  local copies, waits for them, and re-layouts  4.05 us (5%)
    all_gather x3, blocking collectives, merged(): gathered = jax.tree.map(lambda a: lax.all_gather(a, axis), part)  42.2 us
    psum x1, blocking collectives, on_device(): return lax.psum(partial_out, 'head').astype(jnp.bfloat16)  8.73 us
    dot_general x1, matrix products, on_device(): jnp.einsum('sgjd,stgd->sgjt', picked, key_tiles, preferred_element_type=j...  7.04 us
    dot_general x1, matrix products, on_device(): jnp.einsum('sgjt,stgd->sgjd', probs, value_tiles, preferred_element_type=...  4.72 us
    dot_general x1, matrix products, on_device(): jnp.dot(attention, out_weight, preferred_element_type=jnp.float32)  4.59 us
    min x1, other arithmetic, on_device(): jnp.clip(jnp.take(seq_lengths, slot_owner, axis=0) - slot_page * PAGE, 0,...  3.19 us

commit v1 on v0

--- a/solution.py
+++ b/solution.py
@@ -6,6 +6,10 @@
 DH = 128
 PAGE = 128
 neg_fill = -1e30
+
+
+def remake_lots_all(view):
+    return jnp.sum(lax.all_gather(view, "head"), axis=0)
 
 
 def merged(part, axis, combine):
@@ -74,7 +78,7 @@
     top_all, mass_all, out_all = merged((seq_peak, seq_mass, seq_out), ("seq", "sub"), merge_states)
     attention = spread(out_all, 1.0 / mass_all).astype(jnp.bfloat16)
     partial_out = jnp.dot(attention, out_weight, preferred_element_type=jnp.float32)
-    return lax.psum(partial_out, "head").astype(jnp.bfloat16)
+    return remake_lots_all(partial_out).astype(jnp.bfloat16)
 
 
 def solution(mesh):

time: 79.1 us -> 75.4 us (0.953)
  blocking collectives: 50.9 us -> 46.6 us
    psum x1 -> x0, blocking collectives: 8.73 us -> none  [on_device(): return lax.psum(partial_out, 'head').astype(jnp.bfloat16)]
    all_gather x0 -> x1, blocking collectives: none -> 4.4 us  [remake_lots_all(): return jnp.sum(lax.all_gather(view, 'head'), axis=0)]
where the time goes in v1:
time: 75.4 us; the launch traced here: 75.1 us
  blocking collectives  46.6 us (62%)
  matrix products  17.5 us (23%)
  other arithmetic  6.68 us (9%)
  local copies, waits for them, and re-layouts  4.05 us (5%)
    all_gather x3, blocking collectives, merged(): gathered = jax.tree.map(lambda a: lax.all_gather(a, axis), part)  42.2 us
    dot_general x1, matrix products, on_device(): jnp.einsum('sgjd,stgd->sgjt', picked, key_tiles, preferred_element_type=j...  7.04 us
    dot_general x1, matrix products, on_device(): jnp.einsum('sgjt,stgd->sgjd', probs, value_tiles, preferred_element_type=...  4.72 us
    dot_general x1, matrix products, on_device(): jnp.dot(attention, out_weight, preferred_element_type=jnp.float32)  4.59 us
    all_gather x1, blocking collectives, remake_lots_all(): return jnp.sum(lax.all_gather(view, 'head'), axis=0)  4.4 us
    min x1, other arithmetic, on_device(): jnp.clip(jnp.take(seq_lengths, slot_owner, axis=0) - slot_page * PAGE, 0,...  3.19 us

profile of v1, /device:TPU:0, one launch (start us, length us, event | category | flops | bytes accessed | tf_op | source)
XLA Modules:
  0.0 75.1 jit_solution(5350461292194375600)
XLA Ops:
  0.0 1.5 %fusion.39 = (s32[1]{0:T(128)}, s32[1]{0:T(128)}, s32[1]{0:T(128)}, s32[1]{0:T(128)}) fusion(s32[4]{0:T(128)} %param.12), kind=kLoop, calls=%fused_computation.62 | loop fusion | bytes 32 | tf_op jit(solution)/shard_map/jit(_take)/gather | solution.py:52
  1.5 3.2 %fusion.35 = (s32[64]{0:T(128)S(1)}, s32[64]{0:T(128)S(1)}) fusion(s32[64]{0:T(128)} %param.14, s32[]{:T(128)} %bitcast.3, s32[]{:T(128)} %bitcast.4, s32[]{:T(128)} %bitcast.5, s32[]{:T(128)} %bitcast.6, s32[64]{0:T(128)} %param.13), kind=kLoop, calls=%fused_computation.59 | loop fusion | flops 1024 | bytes 1040 | tf_op jit(solution)/shard_map/jit(clip)/min | solution.py:52
  4.7 0.8 %gather_fusion = bf16[64,4096]{1,0:T(8,128)(2,1)S(1)} fusion(bf16[4,4096]{1,0:T(4,128)(2,1)S(1)} %copy-done, s32[1024]{0:T(1024)S(1)} %pad_clamp_fusion), kind=kCustom, calls=%fused_computation | custom fusion | bytes 1048832 | tf_op jit(solution)/shard_map/jit(_take)/gather | solution.py:47
  5.6 0.7 compare_and_fusion
  6.3 7.0 %fusion.40 = (f32[64,4,8]{2,1,0:T(4,128)S(1)}, f32[64,4,8,128]{3,2,1,0:T(8,128)S(1)}) fusion(bf16[64,4,8,128]{3,2,1,0:T(8,128)(2,1)S(1)} %bitcast.108, pred[64]{0:T(512)(128)(4,1)S(1)} %compare_and_fusion, pred[64,128]{1,0:T(8,128)(4,1)S(1)} %iota_compare_fusion, bf16[64,128,512]{2,1,0:T(8,128)(2,1)} %param.10), kind=kOutput, calls=%fused_computation.63 | convolution fusion | flops 68155392 | bytes 9977920 | tf_op jit(solution)/shard_map/sgjd,stgd->sgjt/dot_general | solution.py:50
  13.7 14.5 %all_gather.21 = f32[8,4,32]{2,1,0:T(4,128)S(1)} all-gather(f32[1,4,32]{2,1,0:T(4,128)S(1)} %all_gather_reshape.3), channel_id=1, replica_groups=mesh['rep'=2,'seq'=4,'head'=2,'sub'=2] {'seq','sub'}, dimensions={0}, use_global_device_ids=true | all-gather | bytes 4608 | tf_op jit(solution)/shard_map/all_gather | solution.py:16
  28.2 0.7 gather_fusion.1
  28.9 0.8 %convert_reduce_fusion = f32[64,4,8]{2,1,0:T(4,128)S(1)} fusion(f32[64,4,8,128]{3,2,1,0:T(8,128)S(1)} %get-tuple-element.211, f32[64,4,8]{2,1,0:T(4,128)S(1)} %get-tuple-element.210), kind=kLoop, calls=%fused_computation.27 | loop fusion | flops 1046528 | bytes 1064960 | tf_op jit(solution)/shard_map/reduce_sum | solution.py:58
  29.8 0.1 convolution_bitcast_fusion.2
  29.9 12.8 %all-gather.3 = f32[8,4,32]{2,1,0:T(4,128)S(1)} all-gather(f32[1,4,32]{2,1,0:T(4,128)S(1)} %convolution_bitcast_fusion.2), channel_id=2, replica_groups=mesh['rep'=2,'seq'=4,'head'=2,'sub'=2] {'seq','sub'}, dimensions={0}, use_global_device_ids=true | all-gather | bytes 4608 | tf_op jit(solution)/shard_map/all_gather | solution.py:16
  42.7 0.1 subtract_exponential_fusion.1
  42.8 4.7 %fusion.12 = f32[64,4,8,128]{3,2,1,0:T(8,128)S(1)} fusion(f32[64,4,8]{2,1,0:T(4,128)S(1)} %subtract_exponential_fusion.1, f32[64,4,8,128]{3,2,1,0:T(8,128)S(1)} %get-tuple-element.211, f32[64,4,8]{2,1,0:T(4,128)S(1)} %get-tuple-element.210, bf16[64,128,512]{2,1,0:T(8,128)(2,1)} %param.11), kind=kOutput, calls=%fused_computation.21 | convolution fusion | flops 67895296 | bytes 10502144 | tf_op jit(solution)/shard_map/sgjt,stgd->sgjd/dot_general | solution.py:59
  47.6 1.0 %convolution_bitcast_fusion = f32[1,4,4096]{2,1,0:T(4,128)S(1)} fusion(f32[8,8,32,128]{3,2,1,0:T(8,128)S(1)} %bitcast.110, s32[64]{0:T(128)S(1)} %copy-done.1), kind=kOutput, calls=%fused_computation.19 | convolution fusion | flops 12583168 | bytes 1114368 | tf_op jit(solution)/shard_map/dot_general | solution.py:71
  48.6 14.9 %all-gather.4 = f32[8,4,4096]{2,1,0:T(4,128)S(1)} all-gather(f32[1,4,4096]{2,1,0:T(4,128)S(1)} %convolution_bitcast_fusion), channel_id=3, replica_groups=mesh['rep'=2,'seq'=4,'head'=2,'sub'=2] {'seq','sub'}, dimensions={0}, use_global_device_ids=true | all-gather | bytes 589824 | tf_op jit(solution)/shard_map/all_gather | solution.py:16
  63.5 1.9 %while.19 = (s32[]{:T(128)}, f32[4,32]{1,0:T(4,128)S(1)}, f32[4,32]{1,0:T(4,128)S(1)}, f32[4,4096]{1,0:T(4,128)S(1)}, f32[8,4,32]{2,1,0:T(4,128)S(1)}, /*index=5...) while((s32[]{:T(128)}, f32[4,32]{1,0:T(4,128)S(1)}, ...), condition=%wide.region_4.5_spmd, body=%wide.region_3.4_spmd.sunk | while | flops 49925 | bytes 464023 | solution.py:21
  63.7 0.1 fusion.47
  63.9 0.1 fusion.47
  64.2 0.1 fusion.47
  64.5 0.1 fusion.47
  64.7 0.1 fusion.47
  65.0 0.1 fusion.47
  65.5 4.6 %convolution_bitcast_fusion.1 = f32[1,4,1024]{2,1,0:T(4,128)S(1)} fusion(bf16[4096,1024]{1,0:T(8,128)(2,1)} %param.15, f32[4,4096]{1,0:T(4,128)S(1)} %get-tuple-element.182, f32[1,4,32,128]{3,2,1,0:T(8,128)S(1)} %broadcast_bitcast_fusion.2), kind=kOutput, calls=%fused_computation.23 | convolution fusion | flops 33587200 | bytes 8536064 | tf_op jit(solution)/shard_map/dot_general | solution.py:80
  70.1 4.4 %all-gather.5 = f32[2,4,1024]{2,1,0:T(4,128)S(1)} all-gather(f32[1,4,1024]{2,1,0:T(4,128)S(1)} %convolution_bitcast_fusion.1), channel_id=4, replica_groups=mesh['rep'=2,'seq'=4,'head'=2,'sub'=2] {'head'}, dimensions={0}, use_global_device_ids=true | all-gather | bytes 49152 | tf_op jit(solution)/shard_map/all_gather | solution.py:12
  74.5 0.6 reduce_sum.22
  (33 shorter events, 1.6 us)
Async XLA Ops:
  0.0 4.7 %copy-start = (bf16[4,4096]{1,0:T(4,128)(2,1)S(1)}, bf16[4,4096]{1,0:T(4,128)(2,1)}, u32[]{:S(2)}) copy-start(bf16[4,4096]{1,0:T(4,128)(2,1)} %param.9) | copy-start | bytes 98308
  0.0 13.5 %copy-start.1 = (s32[64]{0:T(128)S(1)}, s32[64]{0:T(128)}, u32[]{:S(2)}) copy-start(s32[64]{0:T(128)} %param.13) | copy-start | bytes 772
